TPU v7x, 32 devices: a whole 2x2x4 slice. The times are simulated.
32 devices in a mesh: gx: 2 (over x), gy: 4 (over y, core), gz: 4 (over z).
Axes of the slice: x: 2, y: 2, z: 4, core: 2. Of those that a mesh axis runs over, the one named last changes fastest.
Arguments:
- ref_pos: float32 [2, 4, 4, 3, 20480], P('gx', 'gy', 'gz'), may hold values from -6 to 6
- step: float32 [2, 4, 4, 3, 20480], P('gx', 'gy', 'gz'), may hold values from -6 to 6
- inv_mass: float32 [2, 4, 4, 20480], P('gx', 'gy', 'gz'), may hold values from 0.08 to 1
- boundary: int32 [2, 4, 4, 1], P('gx', 'gy', 'gz'), may hold values from 0 to 18432, as said below
- bonds: int32 [2, 4, 4, 2, 24416], P('gx', 'gy', 'gz'), may hold values from 0 to 75775, as said below
Outputs:
- positions: float32 [2, 4, 4, 3, 20480], P('gx', 'gy', 'gz')
- max_deviation: float32 [3], replicated
Inputs may be any that keep to these rules, and one draw needn't show every extreme that they name: Each domain's boundary atoms are the 2048 consecutive atoms from boundary on; boundary is a multiple of 2048. In each domain bond c * 127 + m, for the first 20320 bonds, joins atom 128 * c + m to atom 128 * c + m + 1 (chains of 128 consecutive atoms). Cross bond k (bond 20320 + k) joins the domain's boundary atom boundary + (k mod 2048) (first row) to entry k mod 2048 of one of the 26 neighbour blocks of the extended list (second row), never the centre block; which blocks are reached, and how many bonds each one receives, varies from domain to domain. Every such bond is also listed by that neighbour domain with its two ends swapped, the domain's atom then standing in the neighbour's opposite block.
All inputs are finite; a program needn't handle non-finite values.
Results may differ from a plain program's by a relative error of at most 0.00018.
Values sent between devices are 32-bit elements; how exact they have to be, the bound alone decides.
A program may use at most 64 MiB of HBM per device.

v0:
```python
import jax
import jax.numpy as jnp
from jax import lax
from jax.sharding import PartitionSpec as P

ATOMS_DEV = 20480
BOUND = 2048
CROSS_BONDS = 4096
ITERS = 3
LOCAL_BONDS = 20320


relax_factor = 0.7


def with_halo(cells, sides, width):
    for axis, dim in sides:
        count = lax.axis_size(axis)
        head = lax.slice_in_dim(cells, 0, width, axis=dim)
        tail = lax.slice_in_dim(cells, cells.shape[dim] - width, cells.shape[dim], axis=dim)
        cells = jnp.concatenate(
            [
                lax.ppermute(tail, axis, [(i, (i + 1) % count) for i in range(count)]),
                cells,
                lax.ppermute(head, axis, [((i + 1) % count, i) for i in range(count)]),
            ],
            axis=dim,
        )
    return cells


def bond_terms(anchor_left, anchor_right, moved_left, moved_right, inverse_left, inverse_right):
    bond_rest = anchor_left - anchor_right
    bond_now = moved_left - moved_right
    rest_sq = jnp.sum(bond_rest * bond_rest, axis=0)
    now_sq = jnp.sum(bond_now * bond_now, axis=0)
    inner = jnp.sum(bond_rest * bond_now, axis=0)
    excess = now_sq - rest_sq
    deviation = jnp.max(jnp.abs(excess) / (2.0 * jnp.maximum(rest_sq, 1.0)))
    factor = (
        relax_factor * excess / (2.0 * (inverse_left + inverse_right) * jnp.maximum(inner, 1.0))
    )
    return (factor * bond_rest, deviation)


def local(ref_pos, step, inv_mass, boundary, bonds):
    anchor = ref_pos[0, 0, 0]
    current = anchor + step[0, 0, 0]
    inverse = inv_mass[0, 0, 0]
    start = boundary[0, 0, 0, 0]
    chain_count = ATOMS_DEV // 128
    groups = CROSS_BONDS // BOUND
    block_ids = ((bonds[0, 0, 0, 1, LOCAL_BONDS:] - ATOMS_DEV) // BOUND).reshape(groups, BOUND)
    inverse_chain = inverse.reshape(chain_count, 128)
    anchor_chain = anchor.reshape(3, chain_count, 128)
    inverse_slot = lax.dynamic_slice_in_dim(inverse, start, BOUND, 0)
    anchor_slot = lax.dynamic_slice_in_dim(anchor, start, BOUND, 1)

    def rims(values_in):
        return lax.dynamic_slice_in_dim(values_in, start, BOUND, 1)[:, None, None, None, :]

    def spread(blocks):
        return blocks.reshape(blocks.shape[0], 27, BOUND)

    def select(far_rows):
        picked = jnp.zeros((far_rows.shape[0], groups, BOUND), jnp.float32)
        for block in range(27):
            if block == 13:
                continue
            picked = jnp.where((block_ids == block)[None], far_rows[:, block][:, None, :], picked)
        return picked

    fixed = spread(
        with_halo(
            rims(jnp.concatenate([anchor, inverse[None]], axis=0)),
            (("gx", 1), ("gy", 2), ("gz", 3)),
            1,
        )
    )
    far_anchor = fixed[:3]
    far_inverse = fixed[3]
    reports = []
    for iteration in range(ITERS):
        far_moved = spread(with_halo(rims(current), (("gx", 1), ("gy", 2), ("gz", 3)), 1))
        moved_chain = current.reshape(3, chain_count, 128)
        local_term, local_dev = bond_terms(
            anchor_chain[:, :, :-1],
            anchor_chain[:, :, 1:],
            moved_chain[:, :, :-1],
            moved_chain[:, :, 1:],
            inverse_chain[:, :-1],
            inverse_chain[:, 1:],
        )
        zeros_col = jnp.zeros((3, chain_count, 1), jnp.float32)
        delta = jnp.concatenate([-local_term * inverse_chain[:, :-1], zeros_col], axis=2)
        delta = delta + jnp.concatenate([zeros_col, local_term * inverse_chain[:, 1:]], axis=2)
        local_delta, local_dev = (delta.reshape(3, ATOMS_DEV), local_dev)
        moved_slot = lax.dynamic_slice_in_dim(current, start, BOUND, 1)
        term, cross_dev = bond_terms(
            anchor_slot[:, None, :],
            select(far_anchor),
            moved_slot[:, None, :],
            select(far_moved),
            inverse_slot[None, :],
            select(far_inverse[None])[0],
        )
        cross_delta, cross_dev = (-jnp.sum(term, axis=1) * inverse_slot, cross_dev)
        deviation = jnp.maximum(local_dev, cross_dev)
        updated = current + local_delta
        edge_now = lax.dynamic_slice_in_dim(updated, start, BOUND, 1) + cross_delta
        current = lax.dynamic_update_slice_in_dim(updated, edge_now, start, 1)
        reports.append(lax.pmax(deviation, ("gx", "gy", "gz")))
    summary = jnp.stack(reports)
    return (current[None, None, None], summary)


def solution(mesh):
    return jax.shard_map(
        local,
        mesh=mesh,
        in_specs=(
            P("gx", "gy", "gz", None, None),
            P("gx", "gy", "gz", None, None),
            P("gx", "gy", "gz", None),
            P("gx", "gy", "gz", None),
            P("gx", "gy", "gz", None, None),
        ),
        out_specs=(P("gx", "gy", "gz", None, None), P()),
        check_vma=False,
    )
```

profile of v0, /device:TPU:0, one launch (start us, length us, event | category | flops | bytes accessed | tf_op | source)
XLA Modules:
  0.0 154.6 jit_solution(523881820431914745)
XLA Ops:
  1.3 1.2 copy.29
  2.6 3.0 %collective-permute-start.7 = (f32[4,1,1,1,2048]{4,0,3,2,1:T(4,128)S(1)}, f32[4,1,1,1,2048]{4,0,3,2,1:T(4,128)S(1)}, u32[]{:S(2)}, u32[]{:S(2)}) collective-permute-start(f32[4,1,1,1,2048]{4,0,3,2,1:T(4,128)S(1)} %fusion.4), channel_id=1, source_target_pairs={{16,0},{0,16},{17,1},{1,17},{18,2},{2,18},{19,3},{3,19},{20,4},{4,... | collective-permute-start | bytes 98312 | tf_op jit(solution)/shard_map/ppermute | solution.py:25
  6.2 0.5 bitcast_add_fusion.2
  6.8 2.0 %collective-permute-start.1 = (f32[3,1,1,1,2048]{4,0,3,2,1:T(4,128)S(1)}, f32[3,1,1,1,2048]{4,0,3,2,1:T(4,128)S(1)}, u32[]{:S(2)}, u32[]{:S(2)}) collective-permute-start(f32[3,1,1,1,2048]{4,0,3,2,1:T(4,128)S(1)} %fusion.13), channel_id=1, source_target_pairs={{16,0},{0,16},{17,1},{1,17},{18,2},{2,18},{19,3},{3,19},{20,4},{4,... | collective-permute-start | bytes 73736 | tf_op jit(solution)/shard_map/ppermute | solution.py:25
  9.1 0.9 add_reduce_fusion
  10.4 0.7 collective-permute-done.1
  11.1 1.6 %collective-permute-done = f32[3,1,1,1,2048]{4,0,3,2,1:T(4,128)S(1)} collective-permute-done((f32[3,1,1,1,2048]{4,0,3,2,1:T(4,128)S(1)}, f32[3,1,1,1,2048]{4,0,3,2,1:T(4,128)S(1)}, u32[]{:S(2)}, u32[]{:S(2)}) %collective-permute-start) | collective-permute-done | bytes 24608 | tf_op jit(solution)/shard_map/ppermute | solution.py:23
  12.8 0.5 collective-permute-start.2
  13.4 1.4 collective-permute-start.9
  15.0 2.9 %collective-permute-done.2 = f32[3,3,1,1,2048]{4,0,3,2,1:T(4,128)S(1)} collective-permute-done((f32[3,3,1,1,2048]{4,0,3,2,1:T(4,128)S(1)}, f32[3,3,1,1,2048]{4,0,3,2,1:T(4,128)S(1)}, u32[]{:S(2)}, u32[]{:S(2)}) %collective-permute-start.2) | collective-permute-done | bytes 73760 | tf_op jit(solution)/shard_map/ppermute | solution.py:23
  18.1 3.7 %collective-permute-start.5 = (f32[3,3,3,1,2048]{4,0,3,2,1:T(4,128)S(1)}, f32[3,3,3,1,2048]{4,0,3,2,1:T(4,128)S(1)}, u32[]{:S(2)}, u32[]{:S(2)}) collective-permute-start(f32[3,3,3,1,2048]{4,0,3,2,1:T(4,128)S(1)} %pad_maximum_fusion.4), channel_id=1, source_target_pairs={{1,0},{2,1},{3,2},{0,3},{5,4},{6,5},{7,6},{4,7},{9,8},{10,9},{11,1... | collective-permute-start | bytes 663560 | tf_op jit(solution)/shard_map/ppermute | solution.py:25
  21.8 3.9 %collective-permute-start.11 = (f32[4,3,3,1,2048]{4,0,3,2,1:T(4,128)S(1)}, f32[4,3,3,1,2048]{4,0,3,2,1:T(4,128)S(1)}, u32[]{:S(2)}, u32[]{:S(2)}) collective-permute-start(f32[4,3,3,1,2048]{4,0,3,2,1:T(4,128)S(1)} %pad_maximum_fusion.5), channel_id=1, source_target_pairs={{1,0},{2,1},{3,2},{0,3},{5,4},{6,5},{7,6},{4,7},{9,8},{10,9},{11,1... | collective-permute-start | bytes 884744 | tf_op jit(solution)/shard_map/ppermute | solution.py:25
  25.7 3.5 %collective-permute-done.5 = f32[3,3,3,1,2048]{4,0,3,2,1:T(4,128)S(1)} collective-permute-done((f32[3,3,3,1,2048]{4,0,3,2,1:T(4,128)S(1)}, f32[3,3,3,1,2048]{4,0,3,2,1:T(4,128)S(1)}, u32[]{:S(2)}, u32[]{:S(2)}) %collective-permute-start.5) | collective-permute-done | bytes 221216 | tf_op jit(solution)/shard_map/ppermute | solution.py:25
  29.2 7.2 %collective-permute-done.4 = f32[3,3,3,1,2048]{4,0,3,2,1:T(4,128)S(1)} collective-permute-done((f32[3,3,3,1,2048]{4,0,3,2,1:T(4,128)S(1)}, f32[3,3,3,1,2048]{4,0,3,2,1:T(4,128)S(1)}, u32[]{:S(2)}, u32[]{:S(2)}) %collective-permute-start.4) | collective-permute-done | bytes 221216 | tf_op jit(solution)/shard_map/ppermute | solution.py:23
  36.8 5.0 %collective-permute-done.11 = f32[4,3,3,1,2048]{4,0,3,2,1:T(4,128)S(1)} collective-permute-done((f32[4,3,3,1,2048]{4,0,3,2,1:T(4,128)S(1)}, f32[4,3,3,1,2048]{4,0,3,2,1:T(4,128)S(1)}, u32[]{:S(2)}, u32[]{:S(2)}) %collective-permute-start.11) | collective-permute-done | bytes 294944 | tf_op jit(solution)/shard_map/ppermute | solution.py:25
  41.8 6.4 %collective-permute-done.10 = f32[4,3,3,1,2048]{4,0,3,2,1:T(4,128)S(1)} collective-permute-done((f32[4,3,3,1,2048]{4,0,3,2,1:T(4,128)S(1)}, f32[4,3,3,1,2048]{4,0,3,2,1:T(4,128)S(1)}, u32[]{:S(2)}, u32[]{:S(2)}) %collective-permute-start.10) | collective-permute-done | bytes 294944 | tf_op jit(solution)/shard_map/ppermute | solution.py:23
  49.0 1.3 multiply_reduce_fusion.15
  50.3 0.4 multiply_divide_fusion.5
  50.9 0.5 dynamic_update_slice.10
  51.5 0.6 collective-permute-start.13
  52.1 1.5 collective-permute-start.12
  54.0 1.4 collective-permute-done.13
  55.4 0.5 collective-permute-done.12
  56.1 0.5 collective-permute-start.14
  56.8 2.3 %collective-permute-done.15 = f32[3,3,1,1,2048]{4,0,3,2,1:T(4,128)S(1)} collective-permute-done((f32[3,3,1,1,2048]{4,0,3,2,1:T(4,128)S(1)}, f32[3,3,1,1,2048]{4,0,3,2,1:T(4,128)S(1)}, u32[]{:S(2)}, u32[]{:S(2)}) %collective-permute-start.15) | collective-permute-done | bytes 73760 | tf_op jit(solution)/shard_map/ppermute | solution.py:25
  59.1 1.1 collective-permute-done.14
  60.2 1.8 %collective-permute-start.17 = (f32[3,3,3,1,2048]{4,0,3,2,1:T(4,128)S(1)}, f32[3,3,3,1,2048]{4,0,3,2,1:T(4,128)S(1)}, u32[]{:S(2)}, u32[]{:S(2)}) collective-permute-start(f32[3,3,3,1,2048]{4,0,3,2,1:T(4,128)S(1)} %pad_maximum_fusion.6), channel_id=1, source_target_pairs={{1,0},{2,1},{3,2},{0,3},{5,4},{6,5},{7,6},{4,7},{9,8},{10,9},{11,1... | collective-permute-start | bytes 663560 | tf_op jit(solution)/shard_map/ppermute | solution.py:25
  62.4 7.6 %collective-permute-done.17 = f32[3,3,3,1,2048]{4,0,3,2,1:T(4,128)S(1)} collective-permute-done((f32[3,3,3,1,2048]{4,0,3,2,1:T(4,128)S(1)}, f32[3,3,3,1,2048]{4,0,3,2,1:T(4,128)S(1)}, u32[]{:S(2)}, u32[]{:S(2)}) %collective-permute-start.17) | collective-permute-done | bytes 221216 | tf_op jit(solution)/shard_map/ppermute | solution.py:25
  70.0 4.5 %collective-permute-done.16 = f32[3,3,3,1,2048]{4,0,3,2,1:T(4,128)S(1)} collective-permute-done((f32[3,3,3,1,2048]{4,0,3,2,1:T(4,128)S(1)}, f32[3,3,3,1,2048]{4,0,3,2,1:T(4,128)S(1)}, u32[]{:S(2)}, u32[]{:S(2)}) %collective-permute-start.16) | collective-permute-done | bytes 221216 | tf_op jit(solution)/shard_map/ppermute | solution.py:23
  75.1 0.5 multiply_reduce_fusion.12
  75.9 0.5 dynamic_update_slice.11
  76.4 1.4 collective-permute-start.19
  77.9 0.7 collective-permute-start.18
  78.7 0.7 fusion
  79.6 0.9 collective-permute-done.19
  80.4 1.4 collective-permute-done.18
  81.9 0.5 collective-permute-start.20
  82.6 1.5 collective-permute-done.21
  84.1 3.5 %collective-permute-done.20 = f32[3,3,1,1,2048]{4,0,3,2,1:T(4,128)S(1)} collective-permute-done((f32[3,3,1,1,2048]{4,0,3,2,1:T(4,128)S(1)}, f32[3,3,1,1,2048]{4,0,3,2,1:T(4,128)S(1)}, u32[]{:S(2)}, u32[]{:S(2)}) %collective-permute-start.20) | collective-permute-done | bytes 73760 | tf_op jit(solution)/shard_map/ppermute | solution.py:23
  87.7 2.5 %collective-permute-start.23 = (f32[3,3,3,1,2048]{4,0,3,2,1:T(4,128)S(1)}, f32[3,3,3,1,2048]{4,0,3,2,1:T(4,128)S(1)}, u32[]{:S(2)}, u32[]{:S(2)}) collective-permute-start(f32[3,3,3,1,2048]{4,0,3,2,1:T(4,128)S(1)} %pad_maximum_fusion.7), channel_id=1, source_target_pairs={{1,0},{2,1},{3,2},{0,3},{5,4},{6,5},{7,6},{4,7},{9,8},{10,9},{11,1... | collective-permute-start | bytes 663560 | tf_op jit(solution)/shard_map/ppermute | solution.py:25
  90.3 7.4 %collective-permute-done.23 = f32[3,3,3,1,2048]{4,0,3,2,1:T(4,128)S(1)} collective-permute-done((f32[3,3,3,1,2048]{4,0,3,2,1:T(4,128)S(1)}, f32[3,3,3,1,2048]{4,0,3,2,1:T(4,128)S(1)}, u32[]{:S(2)}, u32[]{:S(2)}) %collective-permute-start.23) | collective-permute-done | bytes 221216 | tf_op jit(solution)/shard_map/ppermute | solution.py:25
  97.6 7.4 %collective-permute-done.22 = f32[3,3,3,1,2048]{4,0,3,2,1:T(4,128)S(1)} collective-permute-done((f32[3,3,3,1,2048]{4,0,3,2,1:T(4,128)S(1)}, f32[3,3,3,1,2048]{4,0,3,2,1:T(4,128)S(1)}, u32[]{:S(2)}, u32[]{:S(2)}) %collective-permute-start.22) | collective-permute-done | bytes 221216 | tf_op jit(solution)/shard_map/ppermute | solution.py:23
  105.6 0.5 multiply_reduce_fusion.9
  106.1 0.7 fusion.5
  107.0 0.5 dynamic_update_slice.12
  107.5 0.9 copy.8
  112.1 40.1 %all-reduce.6 = (f32[1]{0:T(128)}, f32[1]{0:T(128)}, f32[1]{0:T(128)}) all-reduce(f32[1]{0:T(128)} %bitcast.149, f32[1]{0:T(128)} %bitcast.148, f32[1]{0:T(128)} %bitcast.147), channel_id=1, replica_groups=mesh['gx'=2,'gy'=4,'gz'=4] {'gx','gy','gz'}, use_global_device_ids=true, to_apply=%region_25.26 | all-reduce | flops 3 | bytes 24 | tf_op jit(solution)/shard_map/pmax | solution.py:112
  152.2 2.4 %pad_maximum_fusion.13 = f32[3]{0:T(128)} fusion(f32[1]{0:T(128)} %get-tuple-element.24, f32[1]{0:T(128)} %get-tuple-element.25, f32[1]{0:T(128)} %get-tuple-element.26), kind=kLoop, calls=%fused_computation.224 | loop fusion | flops 6 | bytes 24 | tf_op jit(solution)/shard_map/stack | solution.py:113
  (79 shorter events, 7.0 us)
Async XLA Ops:
  1.3 1.2 copy-start.1
  1.3 4.4 %copy-start.2 = (f32[1,1,1,3,20480]{4,2,3,1,0:T(1,128)S(1)}, f32[1,1,1,3,20480]{4,2,3,1,0:T(1,128)}, u32[]{:S(2)}) copy-start(f32[1,1,1,3,20480]{4,2,3,1,0:T(1,128)} %param.6) | copy-start | bytes 737284
  2.5 3.3 %copy-start = (f32[1,1,1,3,20480]{4,2,3,1,0:T(1,128)S(1)}, f32[1,1,1,3,20480]{4,2,3,1,0:T(1,128)}, u32[]{:S(2)}) copy-start(f32[1,1,1,3,20480]{4,2,3,1,0:T(1,128)} %param.5) | copy-start | bytes 737284
  2.6 10.7 %collective-permute-start.7 = (f32[4,1,1,1,2048]{4,0,3,2,1:T(4,128)S(1)}, f32[4,1,1,1,2048]{4,0,3,2,1:T(4,128)S(1)}, u32[]{:S(2)}, u32[]{:S(2)}) collective-permute-start(f32[4,1,1,1,2048]{4,0,3,2,1:T(4,128)S(1)} %fusion.4), channel_id=1, source_target_pairs={{16,0},{0,16},{17,1},{1,17},{18,2},{2,18},{19,3},{3,19},{20,4},{4,... | collective-permute-start | bytes 98312 | tf_op jit(solution)/shard_map/ppermute | solution.py:25
  5.6 7.7 %collective-permute-start.6 = (f32[4,1,1,1,2048]{4,0,3,2,1:T(4,128)S(1)}, f32[4,1,1,1,2048]{4,0,3,2,1:T(4,128)S(1)}, u32[]{:S(2)}, u32[]{:S(2)}) collective-permute-start(f32[4,1,1,1,2048]{4,0,3,2,1:T(4,128)S(1)} %fusion.4), channel_id=1, source_target_pairs={{0,16},{16,0},{1,17},{17,1},{2,18},{18,2},{3,19},{19,3},{4,20},{20... | collective-permute-start | bytes 98312 | tf_op jit(solution)/shard_map/ppermute | solution.py:23
  6.8 4.3 %collective-permute-start.1 = (f32[3,1,1,1,2048]{4,0,3,2,1:T(4,128)S(1)}, f32[3,1,1,1,2048]{4,0,3,2,1:T(4,128)S(1)}, u32[]{:S(2)}, u32[]{:S(2)}) collective-permute-start(f32[3,1,1,1,2048]{4,0,3,2,1:T(4,128)S(1)} %fusion.13), channel_id=1, source_target_pairs={{16,0},{0,16},{17,1},{1,17},{18,2},{2,18},{19,3},{3,19},{20,4},{4,... | collective-permute-start | bytes 73736 | tf_op jit(solution)/shard_map/ppermute | solution.py:25
  8.8 3.9 %collective-permute-start = (f32[3,1,1,1,2048]{4,0,3,2,1:T(4,128)S(1)}, f32[3,1,1,1,2048]{4,0,3,2,1:T(4,128)S(1)}, u32[]{:S(2)}, u32[]{:S(2)}) collective-permute-start(f32[3,1,1,1,2048]{4,0,3,2,1:T(4,128)S(1)} %fusion.13), channel_id=1, source_target_pairs={{0,16},{16,0},{1,17},{17,1},{2,18},{18,2},{3,19},{19,3},{4,20},{20... | collective-permute-start | bytes 73736 | tf_op jit(solution)/shard_map/ppermute | solution.py:23
  12.8 2.3 %collective-permute-start.3 = (f32[3,3,1,1,2048]{4,0,3,2,1:T(4,128)S(1)}, f32[3,3,1,1,2048]{4,0,3,2,1:T(4,128)S(1)}, u32[]{:S(2)}, u32[]{:S(2)}) collective-permute-start(f32[3,3,1,1,2048]{4,0,3,2,1:T(4,128)S(1)} %pad_maximum_fusion.9), channel_id=1, source_target_pairs={{4,0},{8,4},{12,8},{0,12},{5,1},{9,5},{13,9},{1,13},{6,2},{10,6},{... | collective-permute-start | bytes 221192 | tf_op jit(solution)/shard_map/ppermute | solution.py:25
  12.8 5.1 %collective-permute-start.2 = (f32[3,3,1,1,2048]{4,0,3,2,1:T(4,128)S(1)}, f32[3,3,1,1,2048]{4,0,3,2,1:T(4,128)S(1)}, u32[]{:S(2)}, u32[]{:S(2)}) collective-permute-start(f32[3,3,1,1,2048]{4,0,3,2,1:T(4,128)S(1)} %pad_maximum_fusion.9), channel_id=1, source_target_pairs={{0,4},{4,8},{8,12},{12,0},{1,5},{5,9},{9,13},{13,1},{2,6},{6,10},{... | collective-permute-start | bytes 221192 | tf_op jit(solution)/shard_map/ppermute | solution.py:23
  13.4 8.3 %collective-permute-start.9 = (f32[4,3,1,1,2048]{4,0,3,2,1:T(4,128)S(1)}, f32[4,3,1,1,2048]{4,0,3,2,1:T(4,128)S(1)}, u32[]{:S(2)}, u32[]{:S(2)}) collective-permute-start(f32[4,3,1,1,2048]{4,0,3,2,1:T(4,128)S(1)} %pad_maximum_fusion.10), channel_id=1, source_target_pairs={{4,0},{8,4},{12,8},{0,12},{5,1},{9,5},{13,9},{1,13},{6,2},{10,6},{... | collective-permute-start | bytes 294920 | tf_op jit(solution)/shard_map/ppermute | solution.py:25
  14.7 7.0 %collective-permute-start.8 = (f32[4,3,1,1,2048]{4,0,3,2,1:T(4,128)S(1)}, f32[4,3,1,1,2048]{4,0,3,2,1:T(4,128)S(1)}, u32[]{:S(2)}, u32[]{:S(2)}) collective-permute-start(f32[4,3,1,1,2048]{4,0,3,2,1:T(4,128)S(1)} %pad_maximum_fusion.10), channel_id=1, source_target_pairs={{0,4},{4,8},{8,12},{12,0},{1,5},{5,9},{9,13},{13,1},{2,6},{6,10},{... | collective-permute-start | bytes 294920 | tf_op jit(solution)/shard_map/ppermute | solution.py:23
  18.1 11.1 %collective-permute-start.5 = (f32[3,3,3,1,2048]{4,0,3,2,1:T(4,128)S(1)}, f32[3,3,3,1,2048]{4,0,3,2,1:T(4,128)S(1)}, u32[]{:S(2)}, u32[]{:S(2)}) collective-permute-start(f32[3,3,3,1,2048]{4,0,3,2,1:T(4,128)S(1)} %pad_maximum_fusion.4), channel_id=1, source_target_pairs={{1,0},{2,1},{3,2},{0,3},{5,4},{6,5},{7,6},{4,7},{9,8},{10,9},{11,1... | collective-permute-start | bytes 663560 | tf_op jit(solution)/shard_map/ppermute | solution.py:25
  21.7 14.7 %collective-permute-start.4 = (f32[3,3,3,1,2048]{4,0,3,2,1:T(4,128)S(1)}, f32[3,3,3,1,2048]{4,0,3,2,1:T(4,128)S(1)}, u32[]{:S(2)}, u32[]{:S(2)}) collective-permute-start(f32[3,3,3,1,2048]{4,0,3,2,1:T(4,128)S(1)} %pad_maximum_fusion.4), channel_id=1, source_target_pairs={{0,1},{1,2},{2,3},{3,0},{4,5},{5,6},{6,7},{7,4},{8,9},{9,10},{10,1... | collective-permute-start | bytes 663560 | tf_op jit(solution)/shard_map/ppermute | solution.py:23
  21.8 20.0 %collective-permute-start.11 = (f32[4,3,3,1,2048]{4,0,3,2,1:T(4,128)S(1)}, f32[4,3,3,1,2048]{4,0,3,2,1:T(4,128)S(1)}, u32[]{:S(2)}, u32[]{:S(2)}) collective-permute-start(f32[4,3,3,1,2048]{4,0,3,2,1:T(4,128)S(1)} %pad_maximum_fusion.5), channel_id=1, source_target_pairs={{1,0},{2,1},{3,2},{0,3},{5,4},{6,5},{7,6},{4,7},{9,8},{10,9},{11,1... | collective-permute-start | bytes 884744 | tf_op jit(solution)/shard_map/ppermute | solution.py:25
  25.7 22.5 %collective-permute-start.10 = (f32[4,3,3,1,2048]{4,0,3,2,1:T(4,128)S(1)}, f32[4,3,3,1,2048]{4,0,3,2,1:T(4,128)S(1)}, u32[]{:S(2)}, u32[]{:S(2)}) collective-permute-start(f32[4,3,3,1,2048]{4,0,3,2,1:T(4,128)S(1)} %pad_maximum_fusion.5), channel_id=1, source_target_pairs={{0,1},{1,2},{2,3},{3,0},{4,5},{5,6},{6,7},{7,4},{8,9},{9,10},{10,1... | collective-permute-start | bytes 884744 | tf_op jit(solution)/shard_map/ppermute | solution.py:23
  51.5 4.0 %collective-permute-start.13 = (f32[3,1,1,1,2048]{4,0,3,2,1:T(4,128)S(1)}, f32[3,1,1,1,2048]{4,0,3,2,1:T(4,128)S(1)}, u32[]{:S(2)}, u32[]{:S(2)}) collective-permute-start(f32[3,1,1,1,2048]{4,0,3,2,1:T(4,128)S(1)} %fusion.12), channel_id=1, source_target_pairs={{16,0},{0,16},{17,1},{1,17},{18,2},{2,18},{19,3},{3,19},{20,4},{4,... | collective-permute-start | bytes 73736 | tf_op jit(solution)/shard_map/ppermute | solution.py:25
  52.1 3.9 %collective-permute-start.12 = (f32[3,1,1,1,2048]{4,0,3,2,1:T(4,128)S(1)}, f32[3,1,1,1,2048]{4,0,3,2,1:T(4,128)S(1)}, u32[]{:S(2)}, u32[]{:S(2)}) collective-permute-start(f32[3,1,1,1,2048]{4,0,3,2,1:T(4,128)S(1)} %fusion.12), channel_id=1, source_target_pairs={{0,16},{16,0},{1,17},{17,1},{2,18},{18,2},{3,19},{19,3},{4,20},{20... | collective-permute-start | bytes 73736 | tf_op jit(solution)/shard_map/ppermute | solution.py:23
  56.0 3.1 %collective-permute-start.15 = (f32[3,3,1,1,2048]{4,0,3,2,1:T(4,128)S(1)}, f32[3,3,1,1,2048]{4,0,3,2,1:T(4,128)S(1)}, u32[]{:S(2)}, u32[]{:S(2)}) collective-permute-start(f32[3,3,1,1,2048]{4,0,3,2,1:T(4,128)S(1)} %pad_maximum_fusion.11), channel_id=1, source_target_pairs={{4,0},{8,4},{12,8},{0,12},{5,1},{9,5},{13,9},{1,13},{6,2},{10,6},{... | collective-permute-start | bytes 221192 | tf_op jit(solution)/shard_map/ppermute | solution.py:25
  56.1 4.1 %collective-permute-start.14 = (f32[3,3,1,1,2048]{4,0,3,2,1:T(4,128)S(1)}, f32[3,3,1,1,2048]{4,0,3,2,1:T(4,128)S(1)}, u32[]{:S(2)}, u32[]{:S(2)}) collective-permute-start(f32[3,3,1,1,2048]{4,0,3,2,1:T(4,128)S(1)} %pad_maximum_fusion.11), channel_id=1, source_target_pairs={{0,4},{4,8},{8,12},{12,0},{1,5},{5,9},{9,13},{13,1},{2,6},{6,10},{... | collective-permute-start | bytes 221192 | tf_op jit(solution)/shard_map/ppermute | solution.py:23
  60.2 9.8 %collective-permute-start.17 = (f32[3,3,3,1,2048]{4,0,3,2,1:T(4,128)S(1)}, f32[3,3,3,1,2048]{4,0,3,2,1:T(4,128)S(1)}, u32[]{:S(2)}, u32[]{:S(2)}) collective-permute-start(f32[3,3,3,1,2048]{4,0,3,2,1:T(4,128)S(1)} %pad_maximum_fusion.6), channel_id=1, source_target_pairs={{1,0},{2,1},{3,2},{0,3},{5,4},{6,5},{7,6},{4,7},{9,8},{10,9},{11,1... | collective-permute-start | bytes 663560 | tf_op jit(solution)/shard_map/ppermute | solution.py:25
  62.0 12.6 %collective-permute-start.16 = (f32[3,3,3,1,2048]{4,0,3,2,1:T(4,128)S(1)}, f32[3,3,3,1,2048]{4,0,3,2,1:T(4,128)S(1)}, u32[]{:S(2)}, u32[]{:S(2)}) collective-permute-start(f32[3,3,3,1,2048]{4,0,3,2,1:T(4,128)S(1)} %pad_maximum_fusion.6), channel_id=1, source_target_pairs={{0,1},{1,2},{2,3},{3,0},{4,5},{5,6},{6,7},{7,4},{8,9},{9,10},{10,1... | collective-permute-start | bytes 663560 | tf_op jit(solution)/shard_map/ppermute | solution.py:23
  76.4 4.0 %collective-permute-start.19 = (f32[3,1,1,1,2048]{4,0,3,2,1:T(4,128)S(1)}, f32[3,1,1,1,2048]{4,0,3,2,1:T(4,128)S(1)}, u32[]{:S(2)}, u32[]{:S(2)}) collective-permute-start(f32[3,1,1,1,2048]{4,0,3,2,1:T(4,128)S(1)} %fusion.11), channel_id=1, source_target_pairs={{16,0},{0,16},{17,1},{1,17},{18,2},{2,18},{19,3},{3,19},{20,4},{4,... | collective-permute-start | bytes 73736 | tf_op jit(solution)/shard_map/ppermute | solution.py:25
  77.9 3.9 %collective-permute-start.18 = (f32[3,1,1,1,2048]{4,0,3,2,1:T(4,128)S(1)}, f32[3,1,1,1,2048]{4,0,3,2,1:T(4,128)S(1)}, u32[]{:S(2)}, u32[]{:S(2)}) collective-permute-start(f32[3,1,1,1,2048]{4,0,3,2,1:T(4,128)S(1)} %fusion.11), channel_id=1, source_target_pairs={{0,16},{16,0},{1,17},{17,1},{2,18},{18,2},{3,19},{19,3},{4,20},{20... | collective-permute-start | bytes 73736 | tf_op jit(solution)/shard_map/ppermute | solution.py:23
  81.8 2.3 %collective-permute-start.21 = (f32[3,3,1,1,2048]{4,0,3,2,1:T(4,128)S(1)}, f32[3,3,1,1,2048]{4,0,3,2,1:T(4,128)S(1)}, u32[]{:S(2)}, u32[]{:S(2)}) collective-permute-start(f32[3,3,1,1,2048]{4,0,3,2,1:T(4,128)S(1)} %pad_maximum_fusion.12), channel_id=1, source_target_pairs={{4,0},{8,4},{12,8},{0,12},{5,1},{9,5},{13,9},{1,13},{6,2},{10,6},{... | collective-permute-start | bytes 221192 | tf_op jit(solution)/shard_map/ppermute | solution.py:25
  81.9 5.8 %collective-permute-start.20 = (f32[3,3,1,1,2048]{4,0,3,2,1:T(4,128)S(1)}, f32[3,3,1,1,2048]{4,0,3,2,1:T(4,128)S(1)}, u32[]{:S(2)}, u32[]{:S(2)}) collective-permute-start(f32[3,3,1,1,2048]{4,0,3,2,1:T(4,128)S(1)} %pad_maximum_fusion.12), channel_id=1, source_target_pairs={{0,4},{4,8},{8,12},{12,0},{1,5},{5,9},{9,13},{13,1},{2,6},{6,10},{... | collective-permute-start | bytes 221192 | tf_op jit(solution)/shard_map/ppermute | solution.py:23
  87.7 9.9 %collective-permute-start.23 = (f32[3,3,3,1,2048]{4,0,3,2,1:T(4,128)S(1)}, f32[3,3,3,1,2048]{4,0,3,2,1:T(4,128)S(1)}, u32[]{:S(2)}, u32[]{:S(2)}) collective-permute-start(f32[3,3,3,1,2048]{4,0,3,2,1:T(4,128)S(1)} %pad_maximum_fusion.7), channel_id=1, source_target_pairs={{1,0},{2,1},{3,2},{0,3},{5,4},{6,5},{7,6},{4,7},{9,8},{10,9},{11,1... | collective-permute-start | bytes 663560 | tf_op jit(solution)/shard_map/ppermute | solution.py:25
  90.2 14.9 %collective-permute-start.22 = (f32[3,3,3,1,2048]{4,0,3,2,1:T(4,128)S(1)}, f32[3,3,3,1,2048]{4,0,3,2,1:T(4,128)S(1)}, u32[]{:S(2)}, u32[]{:S(2)}) collective-permute-start(f32[3,3,3,1,2048]{4,0,3,2,1:T(4,128)S(1)} %pad_maximum_fusion.7), channel_id=1, source_target_pairs={{0,1},{1,2},{2,3},{3,0},{4,5},{5,6},{6,7},{7,4},{8,9},{9,10},{10,1... | collective-permute-start | bytes 663560 | tf_op jit(solution)/shard_map/ppermute | solution.py:23
where the time goes:
time: 155 us
  waiting for transfers between devices  67.2 us (43%)
  blocking collectives  40.1 us (26%)
  starting transfers between devices  24.5 us (16%)
  other arithmetic  12.3 us (8%)
  between operations  5.47 us (4%)
  local copies, waits for them, and re-layouts  5.09 us (3%)
    pmax x1, blocking collectives, local(): reports.append(lax.pmax(deviation, ('gx', 'gy', 'gz')))  40.1 us
    ppermute x12, waiting for transfers between devices, with_halo(): lax.ppermute(tail, axis, [(i, (i + 1) % count) for i in range(count)])  36.6 us
    ppermute x12, waiting for transfers between devices, with_halo(): lax.ppermute(head, axis, [((i + 1) % count, i) for i in range(count)])  30.5 us
    ppermute x12, starting transfers between devices, with_halo(): lax.ppermute(head, axis, [((i + 1) % count, i) for i in range(count)])  20.4 us
    ppermute x12, starting transfers between devices, with_halo(): lax.ppermute(tail, axis, [(i, (i + 1) % count) for i in range(count)])  4.13 us
  transfers between devices with their start and end apart: 24, of which 20 were waited for; matrix products, arithmetic and copies ran while one was open for 3% of the time, Pallas kernels for 0%

commit v1 on v0

v1 whole, which is shorter than its diff:
```python
import functools

import jax
import jax.numpy as jnp
from jax import lax
from jax.experimental import pallas as pl
from jax.experimental.pallas import tpu as pltpu
from jax.sharding import PartitionSpec as P

BOUND = 2048
CROSS_BONDS = 4096
ITERS = 3
CHAIN = 128
RELAX = 0.7
MESH = pl.DeviceIdType.MESH


def offsets(count):
    return (0, 1) if count == 2 else (-1, 0, 1)


def next_lane(x):
    return pltpu.roll(x, CHAIN - 1, x.ndim - 1)


def prev_lane(x):
    return pltpu.roll(x, 1, x.ndim - 1)


def dot3(a, b):
    return a[0] * b[0] + a[1] * b[1] + a[2] * b[2]


def bond_static(rest, weight):
    rest_sq = dot3(rest, rest)
    return rest_sq, 0.5 / jnp.maximum(rest_sq, 1.0), (0.5 * RELAX) / weight


def bond_force(rest, now, static):
    rest_sq, dev_scale, relax = static
    excess = dot3(now, now) - rest_sq
    force = relax * excess / jnp.maximum(dot3(rest, now), 1.0)
    return force, jnp.abs(excess) * dev_scale


def shifted(v, count, stride, off):
    rows = v.shape[0]
    if off == 0 or count == 1:
        return v
    row = lax.broadcasted_iota(jnp.int32, v.shape, 0)
    place = row // stride % count
    if off > 0:
        near = pltpu.roll(v, rows - stride, 0)
        if count * stride == rows:
            return near
        return jnp.where(place < count - 1, near, pltpu.roll(v, (count - 1) * stride, 0))
    near = pltpu.roll(v, stride, 0)
    if count * stride == rows:
        return near
    return jnp.where(place > 0, near, pltpu.roll(v, rows - (count - 1) * stride, 0))


def fetch(planes, codes, grid):
    gx, gy, gz = grid
    picked = [[None] * len(planes) for _ in codes]
    for dz in offsets(gz):
        moved_z = [shifted(v, gz, 1, dz) for v in planes]
        for dy in offsets(gy):
            moved_y = [shifted(v, gy, gz, dy) for v in moved_z]
            for dx in offsets(gx):
                if dx == 0 and dy == 0 and dz == 0:
                    continue
                moved = [shifted(v, gx, gy * gz, dx) for v in moved_y]
                number = float((dx + 1) * 9 + (dy + 1) * 3 + dz + 1)
                for which, code in enumerate(codes):
                    hit = code == number
                    for k, v in enumerate(moved):
                        old = picked[which][k]
                        picked[which][k] = v if old is None else jnp.where(hit, v, old)
    return picked


def chain_setup(anchor, inverse):
    lane = lax.broadcasted_iota(jnp.int32, inverse.shape, 1)
    rest = [a - next_lane(a) for a in anchor]
    static = bond_static(rest, inverse + next_lane(inverse))
    live = lane < CHAIN - 1
    rest_sq, dev_scale, relax = static
    zero = jnp.zeros_like(relax)
    return rest, (rest_sq, jnp.where(live, dev_scale, zero), jnp.where(live, relax, zero))


def chain_delta(moved, rest, static, inverse):
    now = [m - next_lane(m) for m in moved]
    force, dev = bond_force(rest, now, static)
    delta = []
    for c in range(3):
        term = force * rest[c]
        delta.append((prev_lane(term) - term) * inverse)
    return delta, dev


def full_max(x):
    return jnp.max(jnp.max(x, axis=0, keepdims=True), axis=1, keepdims=True)


def dev_row(devs):
    lane = lax.broadcasted_iota(jnp.int32, (1, CHAIN), 1)
    out = jnp.zeros((1, CHAIN), jnp.float32)
    for t, d in enumerate(devs):
        out = jnp.where(lane == t, full_max(d), out)
    return out


def kernel(grid, chains, start_ref, anchor_ref, step_ref, inv_ref, code_ref, out_ref, dev_ref,
           send, recv, res, back, send_sem, recv_sem, ret_sem, back_sem):
    gx, gy, gz = grid
    devices = gx * gy * gz
    share = devices // chains
    me = (lax.axis_index("gx") * gy + lax.axis_index("gy")) * gz + lax.axis_index("gz")
    line = me // gz
    is_owner = line % share == share - 1
    my_chain = line // share * gz + me % gz

    def coords(index):
        return (index // (gy * gz), index // gz % gy, index % gz)

    def owner_of(chain):
        return (chain // gz * share + share - 1) * gz + chain % gz

    barrier = pltpu.get_barrier_semaphore()

    def greet(k, carry):
        other = lax.rem(me + k, devices)
        pl.semaphore_signal(barrier, inc=1, device_id=coords(other), device_id_type=MESH)
        return carry

    lax.fori_loop(1, devices, greet, 0)

    start = jnp.full((chains, CHAIN), start_ref[0], jnp.int32)
    total_rows = inv_ref.shape[0]
    blocks = range(total_rows // chains)
    at = [start == g * BOUND for g in blocks]

    def edge(plane):
        out = plane(pl.ds(0, chains))
        for g in blocks[1:]:
            out = jnp.where(at[g], plane(pl.ds(g * chains, chains)), out)
        return out

    send_flat = send.reshape(send.shape[0] * chains, CHAIN)
    for c in range(3):
        a = edge(lambda rows: anchor_ref[c, rows, :])
        send_flat[c * chains:(c + 1) * chains, :] = a
        send_flat[(3 + c) * chains:(4 + c) * chains, :] = a + edge(lambda rows: step_ref[c, rows, :])
    send_flat[6 * chains:7 * chains, :] = edge(lambda rows: inv_ref[rows, :])
    send_flat[7 * chains:8 * chains, :] = code_ref[0]
    send_flat[8 * chains:9 * chains, :] = code_ref[1]

    group = 2 * chains
    devs = [jnp.zeros((8, CHAIN), jnp.float32)] * ITERS
    for base in range(0, total_rows, group):
        rows = pl.ds(base, group)
        anchor = [anchor_ref[c, rows, :] for c in range(3)]
        inverse = inv_ref[rows, :]
        moved = [anchor[c] + step_ref[c, rows, :] for c in range(3)]
        rest, static = chain_setup(anchor, inverse)
        inner = jnp.concatenate([start != base // chains * BOUND, start != (base // chains + 1) * BOUND], axis=0)
        for t in range(ITERS):
            delta, dev = chain_delta(moved, rest, static, inverse)
            dev = jnp.where(inner, dev, 0.0)
            devs[t] = jnp.maximum(devs[t], jnp.max(dev.reshape(group // 8, 8, CHAIN), axis=0))
            moved = [m + d for m, d in zip(moved, delta)]
        for c in range(3):
            out_ref[c, rows, :] = moved[c]
    send_flat[9 * chains:10 * chains, :] = jnp.broadcast_to(dev_row(devs), (chains, CHAIN))

    pl.semaphore_wait(barrier, devices - 1)

    def forward(chain):
        return pltpu.make_async_remote_copy(
            src_ref=send.at[:, chain], dst_ref=recv.at[:, me],
            send_sem=send_sem.at[chain], recv_sem=recv_sem.at[me],
            device_id=coords(owner_of(chain)), device_id_type=MESH)

    def backward(device):
        return pltpu.make_async_remote_copy(
            src_ref=res.at[:, device], dst_ref=back.at[:, my_chain],
            send_sem=ret_sem.at[device], recv_sem=back_sem.at[my_chain],
            device_id=coords(device), device_id_type=MESH)

    def send_chain(k, carry):
        chain = lax.rem(my_chain + k, chains)

        @pl.when(owner_of(chain) != me)
        def _():
            forward(chain).start()

        return carry

    lax.fori_loop(0, chains, send_chain, 0)

    @pl.when(is_owner)
    def _():
        recv[:, me] = send[:, my_chain]

        def arrive(k, carry):
            other = lax.rem(me + k, devices)
            pltpu.make_async_remote_copy(
                src_ref=send.at[:, 0], dst_ref=recv.at[:, other],
                send_sem=send_sem.at[0], recv_sem=recv_sem.at[other],
                device_id=coords(other), device_id_type=MESH).wait_recv()
            return carry

        lax.fori_loop(1, devices, arrive, 0)
        flat = recv.reshape(recv.shape[0] * devices, CHAIN)
        plane = [flat[k * devices:(k + 1) * devices, :] for k in range(10)]
        anchor, moved, inverse, codes, far_dev = plane[:3], plane[3:6], plane[6], plane[7:9], plane[9]
        rest, static = chain_setup(anchor, inverse)
        far = fetch(anchor + [inverse] + moved, codes, grid)
        cross = []
        for f in far:
            cross_rest = [a - b for a, b in zip(anchor, f[:3])]
            cross.append((cross_rest, bond_static(cross_rest, inverse + f[3])))
        far_moved = [f[4:] for f in far]
        tops = []
        for t in range(ITERS):
            if t:
                far_moved = fetch(moved, codes, grid)
            delta, top = chain_delta(moved, rest, static, inverse)
            for (cross_rest, cross_static), other in zip(cross, far_moved):
                now = [m - o for m, o in zip(moved, other)]
                force, dev = bond_force(cross_rest, now, cross_static)
                top = jnp.maximum(top, dev)
                pull = force * inverse
                delta = [d - pull * r for d, r in zip(delta, cross_rest)]
            moved = [m + d for m, d in zip(moved, delta)]
            tops.append(top)
        row = jnp.maximum(dev_row(tops), jnp.max(far_dev, axis=0, keepdims=True))
        res_flat = res.reshape(4 * devices, CHAIN)
        for c in range(3):
            res_flat[c * devices:(c + 1) * devices, :] = moved[c]
        res_flat[3 * devices:4 * devices, :] = jnp.broadcast_to(row, (devices, CHAIN))

        def give(k, carry):
            backward(lax.rem(me + k, devices)).start()
            return carry

        lax.fori_loop(1, devices, give, 0)
        back[:, my_chain] = res[:, me]

    def collect(k, carry):
        chain = lax.rem(my_chain + k, chains)

        @pl.when(owner_of(chain) != me)
        def _():
            pltpu.make_async_remote_copy(
                src_ref=res.at[:, 0], dst_ref=back.at[:, chain],
                send_sem=ret_sem.at[0], recv_sem=back_sem.at[chain],
                device_id=coords(owner_of(chain)), device_id_type=MESH).wait_recv()
            forward(chain).wait_send()

        return carry

    lax.fori_loop(0, chains, collect, 0)
    back_flat = back.reshape(4 * chains, CHAIN)
    edges = [back_flat[c * chains:(c + 1) * chains, :] for c in range(3)]
    top = jnp.max(back_flat[3 * chains:4 * chains, :], axis=0, keepdims=True)
    dev_ref[...] = jnp.broadcast_to(top, dev_ref.shape)
    for g in blocks:
        rows = pl.ds(g * chains, chains)
        for c in range(3):
            out_ref[c, rows, :] = jnp.where(at[g], edges[c], out_ref[c, rows, :])

    @pl.when(is_owner)
    def _():
        def finish(k, carry):
            backward(lax.rem(me + k, devices)).wait_send()
            return carry

        lax.fori_loop(1, devices, finish, 0)


def local(grid, ref_pos, step, inv_mass, boundary, bonds):
    atoms = ref_pos.shape[-1]
    rows = atoms // CHAIN
    chains = BOUND // CHAIN
    groups = CROSS_BONDS // BOUND
    devices = grid[0] * grid[1] * grid[2]
    ids = (bonds[0, 0, 0, 1, bonds.shape[-1] - CROSS_BONDS:] - atoms) // BOUND
    if grid[0] == 2:
        ids = jnp.where(ids < 9, ids + 18, ids)
    if grid[1] == 2:
        ids = jnp.where(ids // 3 % 3 == 0, ids + 6, ids)
    if grid[2] == 2:
        ids = jnp.where(ids % 3 == 0, ids + 2, ids)
    codes = ids.astype(jnp.float32).reshape(groups, chains, CHAIN)
    vmem = pl.BlockSpec(memory_space=pltpu.VMEM)
    f32 = jnp.float32
    out, dev = pl.pallas_call(
        functools.partial(kernel, grid, chains),
        out_shape=(jax.ShapeDtypeStruct((3, rows, CHAIN), f32),
                   jax.ShapeDtypeStruct((8, CHAIN), f32)),
        in_specs=[pl.BlockSpec(memory_space=pltpu.SMEM)] + [vmem] * 4,
        out_specs=(vmem, vmem),
        scratch_shapes=[
            pltpu.VMEM((10, chains, 1, CHAIN), f32),
            pltpu.VMEM((10, devices, 1, CHAIN), f32),
            pltpu.VMEM((4, devices, 1, CHAIN), f32),
            pltpu.VMEM((4, chains, 1, CHAIN), f32),
            pltpu.SemaphoreType.DMA((chains,)),
            pltpu.SemaphoreType.DMA((devices,)),
            pltpu.SemaphoreType.DMA((devices,)),
            pltpu.SemaphoreType.DMA((chains,)),
        ],
        compiler_params=pltpu.CompilerParams(collective_id=0, has_side_effects=True),
        name="bond_rounds",
    )(boundary[0, 0, 0], ref_pos[0, 0, 0].reshape(3, rows, CHAIN),
      step[0, 0, 0].reshape(3, rows, CHAIN), inv_mass[0, 0, 0].reshape(rows, CHAIN), codes)
    return out.reshape(1, 1, 1, 3, atoms), dev[0, :ITERS]


def solution(mesh):
    grid = (mesh.shape["gx"], mesh.shape["gy"], mesh.shape["gz"])
    return jax.shard_map(
        functools.partial(local, grid),
        mesh=mesh,
        in_specs=(
            P("gx", "gy", "gz", None, None),
            P("gx", "gy", "gz", None, None),
            P("gx", "gy", "gz", None),
            P("gx", "gy", "gz", None),
            P("gx", "gy", "gz", None, None),
        ),
        out_specs=(P("gx", "gy", "gz", None, None), P()),
        check_vma=False,
    )
```

time: 155 us -> 25.1 us (0.16)
  waiting for transfers between devices: 67.2 us -> 0 us
  blocking collectives: 40.1 us -> 0 us
  starting transfers between devices: 24.5 us -> 0 us
  Pallas kernels: 0 us -> 19.3 us
  other arithmetic: 12.3 us -> 1.48 us
  between operations: 5.47 us -> 1.29 us
  local copies, waits for them, and re-layouts: 5.09 us -> 2.84 us
    ppermute x24 -> x0, waiting for transfers between devices: 67.2 us -> none  [the longest x12 36.6 us: with_halo(): lax.ppermute(tail, axis, [(i, (i + 1) % count) for i in range(count)])]
    pmax x1 -> x0, blocking collectives: 40.1 us -> none  [local(): reports.append(lax.pmax(deviation, ('gx', 'gy', 'gz')))]
    ppermute x24 -> x0, starting transfers between devices: 24.5 us -> none  [the longest x12 20.4 us: with_halo(): lax.ppermute(head, axis, [((i + 1) % count, i) for i in range(count)])]
    pallas_call x0 -> x1, Pallas kernels: none -> 19.3 us  [local(): pl.pallas_call(functools.partial(kernel, grid, chains), out_shape=(jax.Sh...]
    reduce_sum x9 -> x0, other arithmetic: 3.05 us -> none  [the longest x2 1.46 us: bond_terms(): rest_sq = jnp.sum(bond_rest * bond_rest, axis=0)]
    another operation x1 -> x0, other arithmetic: 2.38 us -> none  [local(): summary = jnp.stack(reports)]
    concatenate x12 -> x0, other arithmetic: 1.61 us -> none  [with_halo(): jnp.concatenate([lax.ppermute(tail, axis, [(i, (i + 1) % count) for i in...]
  transfers between devices with their start and end apart: 24 -> 0, of which waited for: 20 -> 0; matrix products, arithmetic and copies ran while one was open for 3% -> 0% of each run, Pallas kernels for 0% -> 0%
where the time goes in v1:
time: 25.1 us; the launch traced here: 24.9 us
  Pallas kernels  19.3 us (77%)
  local copies, waits for them, and re-layouts  2.84 us (11%)
  other arithmetic  1.48 us (6%)
  between operations  1.29 us (5%)
    pallas_call x1, Pallas kernels, local(): pl.pallas_call(functools.partial(kernel, grid, chains), out_shape=(jax.Sh...  19.3 us
    unnamed x1, local copies, waits for them, and re-layouts  1.65 us
    squeeze x1, local copies, waits for them, and re-layouts, local(): return (out.reshape(1, 1, 1, 3, atoms), dev[0, :ITERS])  1.19 us
    sub x1, other arithmetic, local(): ids = (bonds[0, 0, 0, 1, bonds.shape[-1] - CROSS_BONDS:] - atoms) // BOUND  0.86 us
    convert_element_type x1, other arithmetic, local(): codes = ids.astype(jnp.float32).reshape(groups, chains, CHAIN)  0.62 us

profile of v1, /device:TPU:0, one launch (start us, length us, event | category | flops | bytes accessed | tf_op | source)
XLA Modules:
  0.0 24.9 jit_solution(12484276346100935406)
XLA Ops:
  1.3 0.9 %slice_add_fusion = s32[1,1,1,1,4096]{4,3,2,1,0:T(1,128)S(1)} fusion(s32[1,1,1,2,24416]{4,3,2,1,0:T(2,128)} %param.9), kind=kLoop, calls=%fused_computation.8 | loop fusion | flops 4096 | bytes 32768 | tf_op jit(solution)/shard_map/sub | solution.py:290
  2.1 0.6 %fusion.1.code_ref = f32[2,16,128]{2,1,0:T(8,128)} fusion(s32[2,16,128]{2,1,0:T(8,128)S(1)} %bitcast.13), kind=kLoop, calls=%fused_computation.6 | loop fusion | flops 77824 | bytes 32768 | tf_op jit(solution)/shard_map/convert_element_type | solution.py:297
  2.8 19.3 %bond_rounds.1 = (f32[3,160,128]{2,1,0:T(8,128)}, f32[8,128]{1,0:T(8,128)}) custom-call(s32[1]{0:T(128)} %bitcast.8.start_ref, f32[3,160,128]{2,1,0:T(8,128)} %bitcast.9, f32[3,160,128]{2,1,0:T(8,128)} %bitcast.10, f32[160,128]{1,0:T(8,128)} %bitcast.12, f32[2,16,128]{2,1,0:T(8,128)} %fusion.1.code_ref), custom_call_target="tpu_custom_call" | custom-call | tf_op jit(solution)/shard_map/bond_rounds/pallas_call | solution.py:300
  22.0 1.2 %slice_bitcast_fusion = f32[3]{0:T(128)} fusion(f32[8,128]{1,0:T(8,128)} %get-tuple-element.5), kind=kLoop, calls=%fused_computation.10 | loop fusion | bytes 24 | tf_op jit(solution)/shard_map/squeeze | solution.py:320
  23.2 1.7 %copy.11 = f32[1,1,1,3,20480]{4,2,3,1,0:T(1,128)} copy(f32[1,1,1,3,20480]{4,2,3,1,0:T(1,128)} %bitcast.11) | data formatting | bytes 491520

commit v2 on v1

v2 whole, which is shorter than its diff:
```python
import functools

import jax
import jax.numpy as jnp
from jax import lax
from jax.experimental import pallas as pl
from jax.experimental.pallas import tpu as pltpu
from jax.sharding import PartitionSpec as P

BOUND = 2048
CROSS_BONDS = 4096
ITERS = 3
CHAIN = 128
RELAX = 0.7
LIMIT = 24 << 20
MESH = pl.DeviceIdType.MESH


def offsets(count):
    return (0, 1) if count == 2 else (-1, 0, 1)


def next_lane(x):
    return pltpu.roll(x, CHAIN - 1, x.ndim - 1)


def prev_lane(x):
    return pltpu.roll(x, 1, x.ndim - 1)


def dot3(a, b):
    return a[0] * b[0] + a[1] * b[1] + a[2] * b[2]


def bond_static(rest, weight):
    rest_sq = dot3(rest, rest)
    return rest_sq, 0.5 / jnp.maximum(rest_sq, 1.0), (0.5 * RELAX) / weight


def bond_force(rest, now, static):
    rest_sq, dev_scale, relax = static
    excess = dot3(now, now) - rest_sq
    force = relax * excess / jnp.maximum(dot3(rest, now), 1.0)
    return force, jnp.abs(excess) * dev_scale


def shifted(v, count, stride, off):
    rows = v.shape[0]
    if off == 0 or count == 1:
        return v
    row = lax.broadcasted_iota(jnp.int32, v.shape, 0)
    place = row // stride % count
    if off > 0:
        near = pltpu.roll(v, rows - stride, 0)
        if count * stride == rows:
            return near
        return jnp.where(place < count - 1, near, pltpu.roll(v, (count - 1) * stride, 0))
    near = pltpu.roll(v, stride, 0)
    if count * stride == rows:
        return near
    return jnp.where(place > 0, near, pltpu.roll(v, rows - (count - 1) * stride, 0))


def fetch(planes, codes, grid):
    gx, gy, gz = grid
    picked = [[None] * len(planes) for _ in codes]
    for dz in offsets(gz):
        moved_z = [shifted(v, gz, 1, dz) for v in planes]
        for dy in offsets(gy):
            moved_y = [shifted(v, gy, gz, dy) for v in moved_z]
            for dx in offsets(gx):
                if dx == 0 and dy == 0 and dz == 0:
                    continue
                moved = [shifted(v, gx, gy * gz, dx) for v in moved_y]
                number = float((dx + 1) * 9 + (dy + 1) * 3 + dz + 1)
                for which, code in enumerate(codes):
                    hit = code == number
                    for k, v in enumerate(moved):
                        old = picked[which][k]
                        picked[which][k] = v if old is None else jnp.where(hit, v, old)
    return picked


def chain_setup(anchor, inverse):
    lane = lax.broadcasted_iota(jnp.int32, inverse.shape, 1)
    rest = [a - next_lane(a) for a in anchor]
    static = bond_static(rest, inverse + next_lane(inverse))
    live = lane < CHAIN - 1
    rest_sq, dev_scale, relax = static
    zero = jnp.zeros_like(relax)
    return rest, (rest_sq, jnp.where(live, dev_scale, zero), jnp.where(live, relax, zero))


def chain_delta(moved, rest, static, inverse):
    now = [m - next_lane(m) for m in moved]
    force, dev = bond_force(rest, now, static)
    delta = []
    for c in range(3):
        term = force * rest[c]
        delta.append((prev_lane(term) - term) * inverse)
    return delta, dev


def full_max(x):
    return jnp.max(jnp.max(x, axis=0, keepdims=True), axis=1, keepdims=True)


def dev_row(devs):
    lane = lax.broadcasted_iota(jnp.int32, (1, CHAIN), 1)
    out = jnp.zeros((1, CHAIN), jnp.float32)
    for t, d in enumerate(devs):
        out = jnp.where(lane == t, full_max(d), out)
    return out


def boundary_codes(ids, atoms, grid):
    code = lax.shift_right_logical(ids - atoms, BOUND.bit_length() - 1)
    if grid[0] == 2:
        code = jnp.where(code < 9, code + 18, code)
    if grid[1] == 2:
        code = jnp.where(lax.rem(lax.div(code, 3), 3) == 0, code + 6, code)
    if grid[2] == 2:
        code = jnp.where(lax.rem(code, 3) == 0, code + 2, code)
    return code.astype(jnp.float32)


def kernel(grid, chains, start_ref, anchor_hbm, step_hbm, inv_hbm, bonds_hbm, bulk_ref, edge_out,
           anchor_ref, step_ref, inv_ref, tail_ref, tail_rows,
           send, recv, res, back, dev_send, dev_recv,
           load_sem, send_sem, recv_sem, dsend_sem, drecv_sem, ret_sem, back_sem):
    gx, gy, gz = grid
    devices = gx * gy * gz
    share = devices // chains
    lines = chains // gz
    mine = [lax.axis_index(n) for n in ("gx", "gy", "gz")]
    line = mine[0] * gy + mine[1]
    me = line * gz + mine[2]
    my_line = lax.div(line, share)
    is_owner = lax.rem(line, share) == share - 1
    my_chain = my_line * gz + mine[2]
    ys = [lax.rem(mine[1] + d, gy) for d in range(gy)]
    zs = [lax.rem(mine[2] + d, gz) for d in range(gz)]
    targets = []
    for i in range(lines):
        to = lax.rem(my_line + i, lines)
        to_line = to * share + share - 1
        x, y = lax.div(to_line, gy), lax.rem(to_line, gy)
        for z in zs:
            targets.append((to * gz + z, (x, y, z)))

    def each_other(act):
        def plane(x, skip):
            for dy, y in enumerate(ys):
                for dz, z in enumerate(zs):
                    if not (skip and dy == 0 and dz == 0):
                        act((x * gy + y) * gz + z, (x, y, z))

        plane(mine[0], True)
        if gx == 2:
            plane(1 - mine[0], False)
        else:
            def step(d, carry):
                plane(lax.rem(mine[0] + d, gx), False)
                return carry

            lax.fori_loop(1, gx, step, 0)

    def each_owner(act):
        for k, (chain, where) in enumerate(targets):
            if k == 0:
                @pl.when(jnp.logical_not(is_owner))
                def _(chain=chain, where=where):
                    act(chain, where)
            else:
                act(chain, where)

    def remote(src, dst, ssem, rsem, where):
        return pltpu.make_async_remote_copy(src_ref=src, dst_ref=dst, send_sem=ssem, recv_sem=rsem,
                                            device_id=where, device_id_type=MESH)

    barrier = pltpu.get_barrier_semaphore()
    each_other(lambda other, where: pl.semaphore_signal(
        barrier, inc=1, device_id=where, device_id_type=MESH))

    lo = bonds_hbm.shape[1] - tail_ref.shape[1]
    loads = [
        pltpu.make_async_copy(bonds_hbm.at[:, pl.ds(lo, tail_ref.shape[1])], tail_ref, load_sem.at[0]),
        pltpu.make_async_copy(anchor_hbm, anchor_ref, load_sem.at[1]),
        pltpu.make_async_copy(step_hbm, step_ref, load_sem.at[2]),
        pltpu.make_async_copy(inv_hbm, inv_ref, load_sem.at[3]),
    ]
    for copy in loads:
        copy.start()

    start = jnp.full((chains, CHAIN), start_ref[0], jnp.int32)
    total_rows = inv_ref.shape[0]
    blocks = range(total_rows // chains)
    at = [start == g * BOUND for g in blocks]

    def edge(plane):
        out = plane(pl.ds(0, chains))
        for g in blocks[1:]:
            out = jnp.where(at[g], plane(pl.ds(g * chains, chains)), out)
        return out

    fields = send.shape[1]
    send_flat = send.reshape(chains * fields, CHAIN)

    def put(k, plane):
        send_flat[pl.ds(k, chains, stride=fields), :] = plane

    loads[0].wait()
    width = tail_ref.shape[1]
    full = width // CHAIN
    tail_rows[...] = jnp.zeros_like(tail_rows)
    for t in range(full):
        tail_rows[t, :] = tail_ref[1, t * CHAIN:(t + 1) * CHAIN]
    if width % CHAIN:
        tail_rows[full, 0:width % CHAIN] = tail_ref[1, full * CHAIN:width]
    shift = width - CROSS_BONDS
    count = 2 * chains
    ids = tail_rows[0:count, :]
    if shift:
        lane = lax.broadcasted_iota(jnp.int32, ids.shape, 1)
        ids = jnp.where(lane < CHAIN - shift, pltpu.roll(ids, CHAIN - shift, 1),
                        pltpu.roll(tail_rows[1:count + 1, :], CHAIN - shift, 1))
    codes = boundary_codes(ids, total_rows * CHAIN, grid)
    put(7, codes[:chains])
    put(8, codes[chains:])
    for copy in loads[1:]:
        copy.wait()
    for c in range(3):
        a = edge(lambda rows: anchor_ref[c, rows, :])
        put(c, a)
        put(3 + c, a + edge(lambda rows: step_ref[c, rows, :]))
    put(6, edge(lambda rows: inv_ref[rows, :]))

    def forward(chain, where):
        return remote(send.at[chain], recv.at[me], send_sem.at[chain], recv_sem.at[me], where)

    def forward_dev(chain, where):
        return remote(dev_send, dev_recv.at[me], dsend_sem.at[chain], drecv_sem.at[me], where)

    def backward(other, where):
        return remote(res.at[other], back.at[my_chain], ret_sem.at[other], back_sem.at[my_chain], where)

    pl.semaphore_wait(barrier, devices - 1)
    each_owner(lambda chain, where: forward(chain, where).start())

    group = 2 * chains
    devs = [jnp.zeros((8, CHAIN), jnp.float32)] * ITERS
    for base in range(0, total_rows, group):
        rows = pl.ds(base, group)
        anchor = [anchor_ref[c, rows, :] for c in range(3)]
        inverse = inv_ref[rows, :]
        moved = [anchor[c] + step_ref[c, rows, :] for c in range(3)]
        rest, static = chain_setup(anchor, inverse)
        inner = jnp.concatenate([start != base // chains * BOUND,
                                 start != (base // chains + 1) * BOUND], axis=0)
        for t in range(ITERS):
            delta, dev = chain_delta(moved, rest, static, inverse)
            dev = jnp.where(inner, dev, 0.0)
            devs[t] = jnp.maximum(devs[t], jnp.max(dev.reshape(group // 8, 8, CHAIN), axis=0))
            moved = [m + d for m, d in zip(moved, delta)]
        for c in range(3):
            bulk_ref[c, rows, :] = moved[c]
    own_dev = dev_row(devs)
    dev_send[...] = own_dev
    each_owner(lambda chain, where: forward_dev(chain, where).start())

    @pl.when(is_owner)
    def _():
        recv[me] = send[my_chain]
        each_other(lambda other, where: remote(
            send.at[0], recv.at[other], send_sem.at[0], recv_sem.at[other], where).wait_recv())
        flat = recv.reshape(devices * fields, CHAIN)
        plane = [flat[pl.ds(k, devices, stride=fields), :] for k in range(fields)]
        anchor, moved, inverse, codes = plane[:3], plane[3:6], plane[6], plane[7:9]
        rest, static = chain_setup(anchor, inverse)
        far = fetch(anchor + [inverse] + moved, codes, grid)
        cross = []
        for f in far:
            cross_rest = [a - b for a, b in zip(anchor, f[:3])]
            cross.append((cross_rest, bond_static(cross_rest, inverse + f[3])))
        far_moved = [f[4:] for f in far]
        tops = []
        for t in range(ITERS):
            if t:
                far_moved = fetch(moved, codes, grid)
            delta, top = chain_delta(moved, rest, static, inverse)
            for (cross_rest, cross_static), other in zip(cross, far_moved):
                now = [m - o for m, o in zip(moved, other)]
                force, dev = bond_force(cross_rest, now, cross_static)
                top = jnp.maximum(top, dev)
                pull = force * inverse
                delta = [d - pull * r for d, r in zip(delta, cross_rest)]
            moved = [m + d for m, d in zip(moved, delta)]
            tops.append(top)
        res_flat = res.reshape(devices * 4, CHAIN)
        for c in range(3):
            res_flat[pl.ds(c, devices, stride=4), :] = moved[c]
        row = jnp.maximum(dev_row(tops), own_dev)
        dev_recv[me] = own_dev
        each_other(lambda other, where: remote(
            dev_send, dev_recv.at[other], dsend_sem.at[0], drecv_sem.at[other], where).wait_recv())
        far_dev = dev_recv.reshape(devices, CHAIN)[...]
        row = jnp.maximum(row, jnp.max(far_dev, axis=0, keepdims=True))
        res_flat[pl.ds(3, devices, stride=4), :] = jnp.broadcast_to(row, (devices, CHAIN))
        each_other(lambda other, where: backward(other, where).start())
        back[my_chain] = res[me]

    each_owner(lambda chain, where: forward(chain, where).wait_send())
    each_owner(lambda chain, where: forward_dev(chain, where).wait_send())
    each_owner(lambda chain, where: remote(
        res.at[0], back.at[chain], ret_sem.at[0], back_sem.at[chain], where).wait_recv())
    back_flat = back.reshape(chains * 4, CHAIN)
    for c in range(4):
        edge_out[c] = back_flat[pl.ds(c, chains, stride=4), :]

    @pl.when(is_owner)
    def _():
        each_other(lambda other, where: backward(other, where).wait_send())


def place(start_ref, bulk_ref, edge_ref, out_ref, dev_ref):
    chains = edge_ref.shape[1]
    start = jnp.full((chains, CHAIN), start_ref[0], jnp.int32)
    for g in range(bulk_ref.shape[1] // chains):
        rows = pl.ds(g * chains, chains)
        for c in range(3):
            out_ref[c, rows, :] = jnp.where(start == g * BOUND, edge_ref[c], bulk_ref[c, rows, :])
    top = jnp.max(edge_ref[3], axis=0, keepdims=True)
    lane = lax.broadcasted_iota(jnp.int32, top.shape, 1)
    for t in range(ITERS):
        dev_ref[t] = jnp.max(jnp.where(lane == t, top, 0.0))


def local(grid, ref_pos, step, inv_mass, boundary, bonds):
    atoms = ref_pos.shape[-1]
    rows = atoms // CHAIN
    chains = BOUND // CHAIN
    devices = grid[0] * grid[1] * grid[2]
    bond_count = bonds.shape[-1]
    tail = bond_count - (bond_count - CROSS_BONDS) // CHAIN * CHAIN
    vmem = pl.BlockSpec(memory_space=pltpu.VMEM)
    smem = pl.BlockSpec(memory_space=pltpu.SMEM)
    hbm = pl.BlockSpec(memory_space=pltpu.HBM)
    f32 = jnp.float32
    dma = pltpu.SemaphoreType.DMA
    start = boundary[0, 0, 0]
    whole = jax.ShapeDtypeStruct((3, rows, CHAIN), f32)
    bulk, edges = pl.pallas_call(
        functools.partial(kernel, grid, chains),
        out_shape=(whole, jax.ShapeDtypeStruct((4, chains, CHAIN), f32)),
        in_specs=[smem] + [hbm] * 4,
        out_specs=(vmem, vmem),
        scratch_shapes=[
            pltpu.VMEM((3, rows, CHAIN), f32),
            pltpu.VMEM((3, rows, CHAIN), f32),
            pltpu.VMEM((rows, CHAIN), f32),
            pltpu.VMEM((2, tail), jnp.int32),
            pltpu.VMEM((tail // CHAIN // 8 * 8 + 8, CHAIN), jnp.int32),
            pltpu.VMEM((chains, 9, 1, CHAIN), f32),
            pltpu.VMEM((devices, 9, 1, CHAIN), f32),
            pltpu.VMEM((devices, 4, 1, CHAIN), f32),
            pltpu.VMEM((chains, 4, 1, CHAIN), f32),
            pltpu.VMEM((1, CHAIN), f32),
            pltpu.VMEM((devices, 1, CHAIN), f32),
            dma((4,)), dma((chains,)), dma((devices,)), dma((chains,)), dma((devices,)),
            dma((devices,)), dma((chains,)),
        ],
        compiler_params=pltpu.CompilerParams(collective_id=0, has_side_effects=True,
                                             vmem_limit_bytes=LIMIT),
        name="bond_rounds",
    )(start, *(pltpu.with_memory_space_constraint(v, pltpu.HBM) for v in (
        ref_pos[0, 0, 0].reshape(3, rows, CHAIN), step[0, 0, 0].reshape(3, rows, CHAIN),
        inv_mass[0, 0, 0].reshape(rows, CHAIN), bonds[0, 0, 0])))
    out, dev = pl.pallas_call(
        place,
        out_shape=(whole, jax.ShapeDtypeStruct((ITERS,), f32)),
        in_specs=[smem, vmem, vmem],
        out_specs=(vmem, smem),
        compiler_params=pltpu.CompilerParams(vmem_limit_bytes=LIMIT),
        name="place_edges",
    )(start, bulk, edges)
    return out.reshape(1, 1, 1, 3, atoms), dev


def solution(mesh):
    grid = (mesh.shape["gx"], mesh.shape["gy"], mesh.shape["gz"])
    return jax.shard_map(
        functools.partial(local, grid),
        mesh=mesh,
        in_specs=(
            P("gx", "gy", "gz", None, None),
            P("gx", "gy", "gz", None, None),
            P("gx", "gy", "gz", None),
            P("gx", "gy", "gz", None),
            P("gx", "gy", "gz", None, None),
        ),
        out_specs=(P("gx", "gy", "gz", None, None), P()),
        check_vma=False,
    )
```

time: 25.1 us -> 20.5 us (0.82)
  local copies, waits for them, and re-layouts: 2.84 us -> 0 us
  other arithmetic: 1.48 us -> 0 us
  Pallas kernels: 19.3 us -> 19 us
    unnamed x1 -> x0, local copies, waits for them, and re-layouts: 1.65 us -> none
    squeeze x1 -> x0, local copies, waits for them, and re-layouts: 1.19 us -> none  [local(): return (out.reshape(1, 1, 1, 3, atoms), dev[0, :ITERS])]
    sub x1 -> x0, other arithmetic: 0.86 us -> none  [local(): ids = (bonds[0, 0, 0, 1, bonds.shape[-1] - CROSS_BONDS:] - atoms) // BOUND]
    convert_element_type x1 -> x0, other arithmetic: 0.62 us -> none  [local(): codes = ids.astype(jnp.float32).reshape(groups, chains, CHAIN)]
    pallas_call x1 -> x2, Pallas kernels: 19.3 us -> 19 us  [the longest x1 18.3 us: local(): pl.pallas_call(functools.partial(kernel, grid, chains), out_shape=(whole,...]
where the time goes in v2:
time: 20.5 us; the launch traced here: 20.3 us
  Pallas kernels  19 us (93%)
  between operations  1.29 us (6%)
    pallas_call x1, Pallas kernels, local(): pl.pallas_call(functools.partial(kernel, grid, chains), out_shape=(whole,...  18.3 us
    pallas_call x1, Pallas kernels, local(): pl.pallas_call(place, out_shape=(whole, jax.ShapeDtypeStruct((ITERS,), f3...  0.72 us

profile of v2, /device:TPU:0, one launch (start us, length us, event | category | flops | bytes accessed | tf_op | source)
XLA Modules:
  0.0 20.3 jit_solution(6016328174656519215)
XLA Ops:
  1.3 18.3 %bond_rounds.1 = (f32[3,160,128]{2,1,0:T(8,128)S(1)}, f32[4,16,128]{2,1,0:T(8,128)S(1)}) custom-call(s32[1]{0:T(128)} %bitcast.6.start_ref, f32[3,160,128]{2,1,0:T(8,128)} %bitcast.8, f32[3,160,128]{2,1,0:T(8,128)} %bitcast.9, f32[160,128]{1,0:T(8,128)} %bitcast.11, s32[2,24416]{1,0:T(2,128)} %bitcast.10), custom_call_target="tpu_custom_call" | custom-call | tf_op jit(solution)/shard_map/bond_rounds/pallas_call | solution.py:352
  19.6 0.7 %place_edges.1 = (f32[3,160,128]{2,1,0:T(8,128)}, f32[3]{0:T(128)}) custom-call(s32[1]{0:T(128)} %bitcast.7.start_ref, f32[3,160,128]{2,1,0:T(8,128)S(1)} %get-tuple-element.6.bulk_ref, f32[4,16,128]{2,1,0:T(8,128)S(1)} %get-tuple-element.7.edge_ref), custom_call_target="tpu_custom_call" | custom-call | tf_op jit(solution)/shard_map/place_edges/pallas_call | solution.py:378

commit v3 on v2

--- a/solution.py
+++ b/solution.py
@@ -130,23 +130,27 @@
            load_sem, send_sem, recv_sem, dsend_sem, drecv_sem, ret_sem, back_sem):
     gx, gy, gz = grid
     devices = gx * gy * gz
-    share = devices // chains
-    lines = chains // gz
+    stride = max(1, gx * gy // chains)
+    lines = gx * gy // stride
+    per = chains // lines
+    first = (gz - per) // 2
     mine = [lax.axis_index(n) for n in ("gx", "gy", "gz")]
     line = mine[0] * gy + mine[1]
     me = line * gz + mine[2]
-    my_line = lax.div(line, share)
-    is_owner = lax.rem(line, share) == share - 1
-    my_chain = my_line * gz + mine[2]
+    my_line = lax.div(line, stride)
+    is_owner = jnp.logical_and(lax.rem(line, stride) == stride - 1,
+                               jnp.logical_and(mine[2] >= first, mine[2] < first + per))
+    my_chain = my_line * per + mine[2] - first
     ys = [lax.rem(mine[1] + d, gy) for d in range(gy)]
     zs = [lax.rem(mine[2] + d, gz) for d in range(gz)]
     targets = []
-    for i in range(lines):
+    for i in reversed(range(lines)):
         to = lax.rem(my_line + i, lines)
-        to_line = to * share + share - 1
+        to_line = to * stride + stride - 1
         x, y = lax.div(to_line, gy), lax.rem(to_line, gy)
-        for z in zs:
-            targets.append((to * gz + z, (x, y, z)))
+        for j in range(per):
+            z = first + lax.rem(mine[2] + j, per)
+            targets.append((i, to * per + z - first, (x, y, z)))
 
     def each_other(act):
         def plane(x, skip):
@@ -166,9 +170,9 @@
             lax.fori_loop(1, gx, step, 0)
 
     def each_owner(act):
-        for k, (chain, where) in enumerate(targets):
-            if k == 0:
-                @pl.when(jnp.logical_not(is_owner))
+        for i, chain, where in targets:
+            if i == 0:
+                @pl.when(jnp.logical_not(jnp.logical_and(is_owner, where[2] == mine[2])))
                 def _(chain=chain, where=where):
                     act(chain, where)
             else:
@@ -179,8 +183,12 @@
                                             device_id=where, device_id_type=MESH)
 
     barrier = pltpu.get_barrier_semaphore()
-    each_other(lambda other, where: pl.semaphore_signal(
-        barrier, inc=1, device_id=where, device_id_type=MESH))
+
+    @pl.when(is_owner)
+    def _():
+        each_other(lambda other, where: pl.semaphore_signal(
+            barrier, inc=1, device_id=where, device_id_type=MESH))
+
 
     lo = bonds_hbm.shape[1] - tail_ref.shape[1]
     loads = [
@@ -244,7 +252,7 @@
     def backward(other, where):
         return remote(res.at[other], back.at[my_chain], ret_sem.at[other], back_sem.at[my_chain], where)
 
-    pl.semaphore_wait(barrier, devices - 1)
+    pl.semaphore_wait(barrier, chains - is_owner.astype(jnp.int32))
     each_owner(lambda chain, where: forward(chain, where).start())
 
     group = 2 * chains

time: 20.5 us -> 19.1 us (0.932)
  Pallas kernels: 19 us -> 17.7 us
    pallas_call x1, Pallas kernels: 18.3 us -> 17 us  [local(): pl.pallas_call(functools.partial(kernel, grid, chains), out_shape=(whole,...]
where the time goes in v3:
time: 19.1 us; the launch traced here: 19 us
  Pallas kernels  17.7 us (93%)
  between operations  1.29 us (7%)
    pallas_call x1, Pallas kernels, local(): pl.pallas_call(functools.partial(kernel, grid, chains), out_shape=(whole,...  17 us
    pallas_call x1, Pallas kernels, local(): pl.pallas_call(place, out_shape=(whole, jax.ShapeDtypeStruct((ITERS,), f3...  0.72 us

profile of v3, /device:TPU:0, one launch (start us, length us, event | category | flops | bytes accessed | tf_op | source)
XLA Modules:
  0.0 19.0 jit_solution(16394984951443183689)
XLA Ops:
  1.3 17.0 %bond_rounds.1 = (f32[3,160,128]{2,1,0:T(8,128)S(1)}, f32[4,16,128]{2,1,0:T(8,128)S(1)}) custom-call(s32[1]{0:T(128)} %bitcast.6.start_ref, f32[3,160,128]{2,1,0:T(8,128)} %bitcast.8, f32[3,160,128]{2,1,0:T(8,128)} %bitcast.9, f32[160,128]{1,0:T(8,128)} %bitcast.11, s32[2,24416]{1,0:T(2,128)} %bitcast.10), custom_call_target="tpu_custom_call" | custom-call | tf_op jit(solution)/shard_map/bond_rounds/pallas_call | solution.py:360
  18.3 0.7 %place_edges.1 = (f32[3,160,128]{2,1,0:T(8,128)}, f32[3]{0:T(128)}) custom-call(s32[1]{0:T(128)} %bitcast.7.start_ref, f32[3,160,128]{2,1,0:T(8,128)S(1)} %get-tuple-element.6.bulk_ref, f32[4,16,128]{2,1,0:T(8,128)S(1)} %get-tuple-element.7.edge_ref), custom_call_target="tpu_custom_call" | custom-call | tf_op jit(solution)/shard_map/place_edges/pallas_call | solution.py:386
